TPU v7x, 512 devices: a 4x2x32 block of a 4x8x32 slice. The times are simulated.
512 devices in a mesh: grp: 2 (over y), seq: 32 (over z), head: 4 (over x), batch: 2 (over core).
Axes of the slice: x: 4, y: 2, z: 32, core: 2. Of those that a mesh axis runs over, the one named last changes fastest.
The devices are a block of a 4x8x32 slice.
Arguments:
- queries: bfloat16 [64, 64, 128], P(('grp', 'batch'), 'head'), parts along dimension 0, may hold values from -8 to 8
- key_cache: bfloat16 [64, 8, 8192, 128], P(('grp', 'batch'), 'head', 'seq'), parts along dimension 0, may hold values from -5 to 5
- value_cache: bfloat16 [64, 8, 8192, 128], P(('grp', 'batch'), 'head', 'seq'), parts along dimension 0, may hold values from -5 to 5
- gate_logits: float32 [2, 64, 64], P(None, ('grp', 'batch'), 'head'), parts along dimension 1, may hold values from -6 to 6
- lengths: int32 [64], P(('grp', 'batch')), parts along dimension 0, may hold values from 2048 to 8192, as said below
- chosen: int32 [64, 8, 16], P(('grp', 'batch'), 'head'), parts along dimension 0, may hold values from 0 to 63, as said below
- counts: int32 [64, 8], P(('grp', 'batch'), 'head'), parts along dimension 0, may hold values from 1 to 16, as said below
Outputs:
- output: bfloat16 [64, 64, 128], P(('grp', 'batch'), 'head'), parts along dimension 0
There are 2 independent parts, one for each index of `grp`. A program takes and returns all parts, laid end to end along the dimension named above; each array names one. Nothing has to cross between parts.
Inputs may be any that keep to these rules, and one draw needn't show every extreme that they name: `lengths`: every draw has a sequence of the full length 8192. `chosen`: for each sequence and key-value head the first counts entries are distinct blocks that start below the sequence's length, and the first entry is block 0; the entries after them are ignored. `counts`: every draw has a sequence with 16 valid entries for every key-value head.
All inputs are finite; a program needn't handle non-finite values.
Results may differ from a plain program's by a relative error of at most 0.02.
Values may be sent and summed in bfloat16 or wider, within the bound.
A program may use at most 64 MiB of HBM per device.

v0:
```python
import math
import jax
import jax.numpy as jnp
from jax import lax
from jax.sharding import PartitionSpec as P

BLOCK = 128


def collected_together(array, axis):
    leaves = jax.tree.leaves(array)
    sequence = sorted(range(len(leaves)), key=lambda k: -leaves[k].size)
    width = (1, *leaves[sequence[0]].shape)[-1]
    lines = [
        jnp.pad(leaves[k].reshape(-1), (0, -leaves[k].size % width)).reshape(-1, width)
        for k in sequence
    ]
    both, at, found = (lax.all_gather(jnp.concatenate(lines), axis), 0, {})
    for k, line in zip(sequence, lines):
        piece = both[:, at : at + len(line)].reshape(len(both), -1)
        found[k] = piece[:, : leaves[k].size].reshape(-1, *leaves[k].shape)
        at += len(line)
    numbers = iter(range(len(leaves)))
    return jax.tree.map(lambda _: found[next(numbers)], array)


def combined_all(array, axis, join):
    gathered = collected_together(
        jax.tree.map(
            lambda a, kind: a.astype(kind), array, (jnp.bfloat16, jnp.bfloat16, jnp.bfloat16)
        ),
        axis,
    )

    def take(source):
        return jax.tree.map(
            lambda a, own: lax.dynamic_index_in_dim(a, source, 0, False).astype(own.dtype),
            gathered,
            array,
        )

    return lax.fori_loop(
        1, lax.axis_size(axis), lambda source, state: join(state, take(source)), take(0)
    )


def softmax_terms(query_rows, key_rows, value_rows, live_mask, score_scale):
    scores = (
        jnp.einsum("pgd,pnd->pgn", query_rows, key_rows, preferred_element_type=jnp.float32)
        * score_scale
    )
    scores = jnp.where(live_mask[:, None, :], scores, -1e30)
    row_max = jnp.max(scores, axis=2)
    weights = jnp.where(live_mask[:, None, :], jnp.exp(scores - row_max[:, :, None]), 0.0)
    weight_sum = jnp.sum(weights, axis=2)
    summed = jnp.einsum(
        "pgn,pnd->pgd", weights.astype(jnp.bfloat16), value_rows, preferred_element_type=jnp.float32
    )
    return (row_max, weight_sum, summed)


def combine(first, second):
    merged = []
    for index in range(0, len(first), 3):
        row_max = jnp.maximum(first[index], second[index])
        factor_first = jnp.exp(first[index] - row_max)
        factor_second = jnp.exp(second[index] - row_max)
        merged.append(row_max)
        merged.append(first[index + 1] * factor_first + second[index + 1] * factor_second)
        merged.append(
            first[index + 2] * factor_first[:, :, None]
            + second[index + 2] * factor_second[:, :, None]
        )
    return tuple(merged)


def finish(weight_sum, summed):
    return summed / weight_sum[:, :, None]


def pool_blocks(key_rows, value_rows, pair_lengths, first_block):
    pair_count, tokens, head_width = key_rows.shape
    block_count = tokens // BLOCK
    position = first_block * BLOCK + jnp.arange(tokens, dtype=jnp.int32)
    live_mask = position[None, :] < pair_lengths[:, None]
    token_ones = live_mask.astype(jnp.bfloat16).reshape(pair_count, block_count, BLOCK)
    starts = (first_block + jnp.arange(block_count, dtype=jnp.int32)) * BLOCK
    filled = jnp.clip(pair_lengths[:, None] - starts[None, :], 0, BLOCK)
    root_fill = jnp.sqrt(jnp.maximum(filled, 1).astype(jnp.float32))[:, :, None]
    key_sums = jnp.einsum(
        "pjt,pjtd->pjd",
        token_ones,
        key_rows.reshape(pair_count, block_count, BLOCK, head_width),
        preferred_element_type=jnp.float32,
    )
    value_sums = jnp.einsum(
        "pjt,pjtd->pjd",
        token_ones,
        value_rows.reshape(pair_count, block_count, BLOCK, head_width),
        preferred_element_type=jnp.float32,
    )
    pooled_keys = (key_sums / root_fill).astype(jnp.bfloat16)
    pooled_values = (value_sums / root_fill).astype(jnp.bfloat16)
    return (live_mask, filled > 0, pooled_keys, pooled_values)


def picked_tokens(live_mask, chosen_rows, count_rows, first_block):
    pair_count, tokens = live_mask.shape
    block_count = tokens // BLOCK
    block_ids = first_block + jnp.arange(block_count, dtype=jnp.int32)
    slot_live = jnp.arange(chosen_rows.shape[1], dtype=jnp.int32)[None, :] < count_rows[:, None]
    picked = jnp.any(
        (chosen_rows[:, :, None] == block_ids[None, None, :]) & slot_live[:, :, None], axis=1
    )
    spread = jnp.broadcast_to(picked[:, :, None], (pair_count, block_count, BLOCK)).reshape(
        pair_count, tokens
    )
    return live_mask & spread


def blend_gates(compressed, selected, gate_pairs):
    mixed = gate_pairs[0][:, :, None] * compressed + gate_pairs[1][:, :, None] * selected
    return mixed.astype(jnp.bfloat16)


def on_device(queries, key_cache, value_cache, gate_logits, lengths, chosen, counts):
    batch_rows, head_count, context, head_width = key_cache.shape
    pair_count = batch_rows * head_count
    group_size = queries.shape[1] // head_count
    score_scale = 1.0 / math.sqrt(head_width)
    query_rows = queries.reshape(pair_count, group_size, head_width)
    pair_keys = key_cache.reshape(pair_count, context, head_width)
    pair_values = value_cache.reshape(pair_count, context, head_width)
    pair_lengths = jnp.broadcast_to(lengths[:, None], (batch_rows, head_count)).reshape(pair_count)
    pair_chosen = chosen.reshape(pair_count, chosen.shape[2])
    pair_counts = counts.reshape(pair_count)
    gate_pairs = jax.nn.sigmoid(gate_logits.reshape(2, pair_count, group_size))
    local_blocks = context // BLOCK
    first_block = lax.axis_index("seq") * local_blocks
    live_mask, block_live, pooled_keys, pooled_values = pool_blocks(
        pair_keys, pair_values, pair_lengths, first_block
    )
    token_mask = picked_tokens(live_mask, pair_chosen, pair_counts, first_block)
    all_keys, all_values = (
        lax.all_gather(pooled_keys, "seq", axis=1, tiled=True),
        lax.all_gather(pooled_values, "seq", axis=1, tiled=True),
    )
    all_starts = jnp.arange(all_keys.shape[1], dtype=jnp.int32) * BLOCK
    all_live = all_starts[None, :] < pair_lengths[:, None]
    s_max, s_sum, s_val = softmax_terms(query_rows, pair_keys, pair_values, token_mask, score_scale)
    merged = combined_all((s_max, s_sum, s_val), "seq", combine)
    c_max, c_sum, c_val = softmax_terms(query_rows, all_keys, all_values, all_live, score_scale)
    output = blend_gates(finish(c_sum, c_val), finish(merged[1], merged[2]), gate_pairs)
    return output.reshape(batch_rows, head_count * group_size, head_width)


def solution(mesh):
    return jax.shard_map(
        on_device,
        mesh=mesh,
        in_specs=(
            P(("grp", "batch"), "head", None),
            P(("grp", "batch"), "head", "seq", None),
            P(("grp", "batch"), "head", "seq", None),
            P(None, ("grp", "batch"), "head"),
            P(("grp", "batch")),
            P(("grp", "batch"), "head", None),
            P(("grp", "batch"), "head"),
        ),
        out_specs=P(("grp", "batch"), "head", None),
        check_vma=False,
    )
```

profile of v0, /device:TPU:36, one launch (start us, length us, event | category | flops | bytes accessed | tf_op | source)
XLA Modules:
  0.0 226.8 jit_solution(120527223969621659)
XLA Ops:
  6.6 0.9 broadcast_in_dim.71
  7.4 0.1 lt.87
  7.5 0.8 copy.48
  8.3 0.1 lt.97
  8.4 0.8 copy.47
  9.2 0.1 and_reduce_fusion
  9.3 0.1 copy.49
  9.4 0.1 broadcast_in_dim.76
  9.6 1.7 fusion.34
  11.3 0.2 fusion.16
  11.5 0.4 fusion.13
  11.9 0.1 convert_element_type.106
  12.0 0.1 convert_element_type.104
  12.1 0.6 maximum_bitcast_fusion
  13.2 0.1 compare_bitcast_fusion
  13.3 2.3 fusion.22
  15.6 0.7 fusion.24
  16.2 0.1 fusion.29
  16.3 98.2 %all_gather.12 = bf16[32,64,128]{2,0,1:T(8,128)(2,1)S(1)} all-gather(bf16[32,2,128]{2,0,1:T(8,128)(2,1)S(1)} %get-tuple-element.236), channel_id=1, replica_groups=mesh['grp'=2,'seq'=32,'head'=4,'batch'=2] {'seq'}, dimensions={1}, use_global_device_ids=true | all-gather | bytes 540672 | tf_op jit(solution)/shard_map/all_gather | solution.py:145
  114.5 0.6 fusion.35
  115.1 54.7 %all_gather.13 = bf16[32,64,128]{2,0,1:T(8,128)(2,1)S(1)} all-gather(bf16[32,2,128]{2,0,1:T(8,128)(2,1)S(1)} %get-tuple-element.237), channel_id=1, replica_groups=mesh['grp'=2,'seq'=32,'head'=4,'batch'=2] {'seq'}, dimensions={1}, use_global_device_ids=true | all-gather | bytes 540672 | tf_op jit(solution)/shard_map/all_gather | solution.py:146
  169.8 5.3 %all-gather.4.cloned.1.call-done = bf16[32,260,128]{2,1,0:T(8,128)(2,1)} async-done(((bf16[1,260,128]{2,1,0:T(8,128)(2,1)}), bf16[32,260,128]{2,1,0:T(8,128)(2,1)}) %all-gather.4.cloned.1.call-update) | async-done | bytes 2129936 | tf_op jit(solution)/shard_map/all_gather | solution.py:18
  175.1 0.9 fusion.32
  176.1 0.1 copy.60
  176.2 0.1 copy.54
  176.3 0.1 copy.61
  176.5 0.1 copy.55
  176.6 0.8 slice_convert_fusion
  177.6 0.1 copy.53
  177.7 3.1 %slice_bitcast_fusion = bf16[32,32,8,128]{3,2,1,0:T(8,128)(2,1)} fusion(bf16[32,260,128]{2,1,0:T(8,128)(2,1)} %all-gather.4.cloned.1.call-done), kind=kLoop, calls=%fused_computation.9 | loop fusion | bytes 4194304 | tf_op jit(solution)/shard_map/reshape;reshape | solution.py:21
  180.8 0.8 fusion.26
  181.7 37.2 %while.19 = (s32[]{:T(128)}, f32[32,8]{0,1:T(8,128)S(1)}, f32[32,8]{0,1:T(8,128)S(1)}, f32[32,8,128]{2,1,0:T(8,128)S(1)}, bf16[32,32,8]{1,2,0:T(8,128)(2,1)S(1)}...) while((s32[]{:T(128)}, f32[32,8]{0,1:T(8,128)S(1)}, ...), condition=%wide.region_6.7_spmd, body=%wide.region_5.6_spmd.sunk | while | flops 133125 | bytes 341143 | solution.py:42
  181.9 1.0 fusion.48
  183.1 1.0 fusion.48
  184.3 1.0 fusion.48
  185.5 1.0 fusion.48
  186.7 1.0 fusion.48
  187.9 1.0 fusion.48
  189.1 1.0 fusion.48
  190.3 1.0 fusion.48
  191.5 1.0 fusion.48
  192.7 1.0 fusion.48
  193.9 1.0 fusion.48
  195.1 1.0 fusion.48
  196.3 1.0 fusion.48
  197.5 1.0 fusion.48
  198.7 1.0 fusion.48
  199.9 1.0 fusion.48
  201.1 1.0 fusion.48
  202.3 1.0 fusion.48
  203.5 1.0 fusion.48
  204.7 1.0 fusion.48
  205.9 1.0 fusion.48
  207.1 1.0 fusion.48
  208.3 1.0 fusion.48
  209.5 1.0 fusion.48
  210.7 1.0 fusion.48
  211.9 1.0 fusion.48
  213.1 1.0 fusion.48
  214.3 1.0 fusion.48
  215.5 1.0 fusion.48
  216.7 1.0 fusion.48
  217.9 1.0 fusion.48
  219.0 0.9 fusion.12
  (120 shorter events, 6.0 us)
Async XLA Ops:
  6.5 3.0 %copy-start = (bf16[16,2,256,128]{3,2,1,0:T(8,128)(2,1)S(1)}, bf16[16,2,256,128]{3,2,1,0:T(8,128)(2,1)}, u32[]{:S(2)}) copy-start(bf16[16,2,256,128]{3,2,1,0:T(8,128)(2,1)} %param.10) | copy-start | bytes 6291460
  6.6 168.6 %all-gather.4.cloned.1.call-start = ((), (), s32[]{:S(2)}) async-start(), calls=%async_computation | async-start | bytes 2230272 | tf_op jit(solution)/shard_map/all_gather | solution.py:18
  9.4 2.1 copy-start.1
  11.3 1.6 copy-start.3
  13.3 101.2 %copy-start.2 = (bf16[16,16,128]{2,1,0:T(8,128)(2,1)S(1)}, bf16[16,16,128]{2,1,0:T(8,128)(2,1)}, u32[]{:S(2)}) copy-start(bf16[16,16,128]{2,1,0:T(8,128)(2,1)} %param.9) | copy-start | bytes 196612
Sparse Core Ops, SparseCore 0:
  13.0 162.1 all-gather.3
where the time goes:
time: 229 us; the launch traced here: 227 us
  blocking collectives  153 us (67%)
  other arithmetic  34.5 us (15%)
  between operations  13.6 us (6%)
  local copies, waits for them, and re-layouts  12.8 us (6%)
  matrix products  6.53 us (3%)
  waiting for transfers between devices  5.39 us (2%)
    all_gather x1, blocking collectives, on_device(): lax.all_gather(pooled_keys, 'seq', axis=1, tiled=True)  98.2 us
    all_gather x1, blocking collectives, on_device(): lax.all_gather(pooled_values, 'seq', axis=1, tiled=True)  54.7 us
    add x31, other arithmetic, combine(): first[index + 2] * factor_first[:, :, None]  31 us
    all_gather x1, waiting for transfers between devices, collected_together(): both, at, found = (lax.all_gather(jnp.concatenate(lines), axis), 0, {})  5.34 us
  transfers between devices with their start and end apart: 1, of which 1 were waited for; matrix products, arithmetic and copies ran while one was open for 2% of the time, Pallas kernels for 0%

commit v1 on v0

--- a/solution.py
+++ b/solution.py
@@ -5,6 +5,13 @@
 from jax.sharding import PartitionSpec as P
 
 BLOCK = 128
+
+
+def all_by_exchange(value, name, dim):
+    size = lax.axis_size(name)
+    tiles = jnp.stack([value for _ in range(size)])
+    tiles = lax.all_to_all(tiles, name, split_axis=0, concat_axis=0)
+    return jnp.concatenate(tiles, axis=dim)
 
 
 def collected_together(array, axis):
@@ -142,7 +149,7 @@
     )
     token_mask = picked_tokens(live_mask, pair_chosen, pair_counts, first_block)
     all_keys, all_values = (
-        lax.all_gather(pooled_keys, "seq", axis=1, tiled=True),
+        all_by_exchange(pooled_keys, "seq", 1),
         lax.all_gather(pooled_values, "seq", axis=1, tiled=True),
     )
     all_starts = jnp.arange(all_keys.shape[1], dtype=jnp.int32) * BLOCK

time: 229 us -> 261 us (1.14)
  the two profiles are of different devices: /device:TPU:36 before, /device:TPU:38 now
where the time goes in v1:
time: 261 us; the launch traced here: 259 us
  blocking collectives  97.9 us (38%)
  starting transfers between devices  45.8 us (18%)
  waiting for transfers between devices  45 us (17%)
  other arithmetic  34.6 us (13%)
  local copies, waits for them, and re-layouts  14.8 us (6%)
  between operations  13.6 us (5%)
  matrix products  6.57 us (3%)
    all_gather x1, blocking collectives, on_device(): lax.all_gather(pooled_values, 'seq', axis=1, tiled=True)  97.9 us
    all_to_all x1, starting transfers between devices, all_by_exchange(): tiles = lax.all_to_all(tiles, name, split_axis=0, concat_axis=0)  45.8 us
    all_gather x1, waiting for transfers between devices, collected_together(): both, at, found = (lax.all_gather(jnp.concatenate(lines), axis), 0, {})  45 us
    add x31, other arithmetic, combine(): first[index + 2] * factor_first[:, :, None]  31 us
  transfers between devices with their start and end apart: 2, of which 1 were waited for; matrix products, arithmetic and copies ran while one was open for 2% of the time, Pallas kernels for 0%

profile of v1, /device:TPU:38, one launch (start us, length us, event | category | flops | bytes accessed | tf_op | source)
XLA Modules:
  0.0 259.4 jit_solution(4051450664538254495)
XLA Ops:
  6.6 0.9 broadcast_in_dim.71
  7.4 0.1 lt.87
  7.5 0.1 compare_bitcast_fusion
  7.7 2.2 fusion.21
  9.9 0.6 fusion.23
  10.6 0.1 fusion.28
  10.8 1.3 stack.2
  12.0 45.8 %all-to-all-start = ((bf16[32,32,2,128]{3,2,1,0:T(2,128)(2,1)}), bf16[32,32,2,128]{3,2,1,0:T(2,128)(2,1)S(1)}, u32[]{:S(2)}, u32[]{:S(2)}) async-start(bf16[32,32,2,128]{3,2,1,0:T(2,128)(2,1)} %stack.2), calls=%async_computation | async-start | bytes 1048576 | tf_op jit(solution)/shard_map/all_to_all | solution.py:13
  58.0 0.1 lt.97
  58.2 0.1 and_reduce_fusion
  58.3 0.1 copy.51
  58.4 0.1 broadcast_in_dim.76
  58.6 0.7 fusion.33
  59.3 0.7 copy-done.1
  60.0 0.4 fusion.13
  60.4 0.2 fusion.15
  60.6 0.1 convert_element_type.106
  60.7 0.1 convert_element_type.104
  60.8 0.6 maximum_bitcast_fusion
  61.8 97.9 %all_gather.9 = bf16[32,64,128]{2,0,1:T(8,128)(2,1)S(1)} all-gather(bf16[32,2,128]{2,0,1:T(8,128)(2,1)S(1)} %get-tuple-element.237), channel_id=1, replica_groups=mesh['grp'=2,'seq'=32,'head'=4,'batch'=2] {'seq'}, dimensions={1}, use_global_device_ids=true | all-gather | bytes 540672 | tf_op jit(solution)/shard_map/all_gather | solution.py:153
  159.8 1.4 copy.47
  161.1 1.6 fusion.34
  162.7 45.0 %all-gather.4.cloned.1.call-done = bf16[32,260,128]{2,1,0:T(8,128)(2,1)} async-done(((bf16[1,260,128]{2,1,0:T(8,128)(2,1)}), bf16[32,260,128]{2,1,0:T(8,128)(2,1)}) %all-gather.4.cloned.1.call-update) | async-done | bytes 2129936 | tf_op jit(solution)/shard_map/all_gather | solution.py:25
  207.7 0.9 fusion.31
  208.6 0.1 copy.62
  208.8 0.1 copy.56
  208.9 0.1 copy.63
  209.0 0.1 copy.57
  209.2 0.7 slice_convert_fusion
  210.2 3.2 %slice_bitcast_fusion = bf16[32,32,8,128]{3,2,1,0:T(8,128)(2,1)} fusion(bf16[32,260,128]{2,1,0:T(8,128)(2,1)} %all-gather.4.cloned.1.call-done), kind=kLoop, calls=%fused_computation.9 | loop fusion | bytes 4194304 | tf_op jit(solution)/shard_map/reshape;reshape | solution.py:28
  213.4 0.8 fusion.25
  214.2 37.3 %while.19 = (s32[]{:T(128)}, f32[32,8]{0,1:T(8,128)S(1)}, f32[32,8]{0,1:T(8,128)S(1)}, f32[32,8,128]{2,1,0:T(8,128)S(1)}, bf16[32,32,8]{1,2,0:T(8,128)(2,1)S(1)}...) while((s32[]{:T(128)}, f32[32,8]{0,1:T(8,128)S(1)}, ...), condition=%wide.region_6.7_spmd, body=%wide.region_5.6_spmd.sunk | while | flops 133125 | bytes 341143 | solution.py:49
  214.4 1.0 fusion.46
  215.6 1.0 fusion.46
  216.8 1.0 fusion.46
  218.0 1.0 fusion.46
  219.2 1.0 fusion.46
  220.4 1.0 fusion.46
  221.6 1.0 fusion.46
  222.8 1.0 fusion.46
  224.0 1.0 fusion.46
  225.2 1.0 fusion.46
  226.4 1.0 fusion.46
  227.6 1.0 fusion.46
  228.8 1.0 fusion.46
  230.0 1.0 fusion.46
  231.2 1.0 fusion.46
  232.4 1.0 fusion.46
  233.6 1.0 fusion.46
  234.8 1.0 fusion.46
  236.1 1.0 fusion.46
  237.3 1.0 fusion.46
  238.5 1.0 fusion.46
  239.7 1.0 fusion.46
  240.9 1.0 fusion.46
  242.1 1.0 fusion.46
  243.3 1.0 fusion.46
  244.5 1.0 fusion.46
  245.7 1.0 fusion.46
  246.9 1.0 fusion.46
  248.1 1.0 fusion.46
  249.3 1.0 fusion.46
  250.5 1.0 fusion.46
  251.6 0.9 fusion.12
  (128 shorter events, 6.4 us)
Async XLA Ops:
  6.5 3.3 %copy-start = (bf16[16,2,256,128]{3,2,1,0:T(8,128)(2,1)S(1)}, bf16[16,2,256,128]{3,2,1,0:T(8,128)(2,1)}, u32[]{:S(2)}) copy-start(bf16[16,2,256,128]{3,2,1,0:T(8,128)(2,1)} %param.10) | copy-start | bytes 6291460
  9.9 48.0 %copy-start.5 = (s32[16,2]{0,1:T(2,128)S(1)}, s32[16,2]{0,1:T(2,128)}, u32[]{:S(2)}) copy-start(s32[16,2]{0,1:T(2,128)} %param.15) | copy-start | bytes 388
  9.9 48.2 %copy-start.3 = (s32[16,2,16]{2,1,0:T(2,128)S(1)}, s32[16,2,16]{2,1,0:T(2,128)}, u32[]{:S(2)}) copy-start(s32[16,2,16]{2,1,0:T(2,128)} %param.14) | copy-start | bytes 6148
  9.9 48.7 %copy-start.2 = (bf16[16,16,128]{2,1,0:T(8,128)(2,1)S(1)}, bf16[16,16,128]{2,1,0:T(8,128)(2,1)}, u32[]{:S(2)}) copy-start(bf16[16,16,128]{2,1,0:T(8,128)(2,1)} %param.9) | copy-start | bytes 196612
  12.0 147.7 %all-to-all-start = ((bf16[32,32,2,128]{3,2,1,0:T(2,128)(2,1)}), bf16[32,32,2,128]{3,2,1,0:T(2,128)(2,1)S(1)}, u32[]{:S(2)}, u32[]{:S(2)}) async-start(bf16[32,32,2,128]{3,2,1,0:T(2,128)(2,1)} %stack.2), calls=%async_computation | async-start | bytes 1048576 | tf_op jit(solution)/shard_map/all_to_all | solution.py:13
  57.8 149.9 %all-gather.4.cloned.1.call-start = ((), (), s32[]{:S(2)}) async-start(), calls=%async_computation.1 | async-start | bytes 2230272 | tf_op jit(solution)/shard_map/all_gather | solution.py:25
  58.4 1.6 copy-start.1
  59.3 2.2 copy-start.4
Sparse Core Ops, SparseCore 0:
  61.7 145.9 all-gather.3
